TPU v7x, 32 devices: a whole 2x2x4 slice. The times are simulated.
32 devices in a mesh: row: 4 (over x, core), col: 4 (over z), layer: 2 (over y).
Axes of the slice: x: 2, y: 2, z: 4, core: 2. Of those that a mesh axis runs over, the one named last changes fastest.
Arguments:
- attn_values: bfloat16 [2048, 8192], P('row', ('layer', 'col')), may hold values from -6 to 6
- out_weight: bfloat16 [8192, 8192], P(('layer', 'row'), 'col'), may hold values from -0.09375 to 0.09375
Outputs:
- projected: bfloat16 [2048, 8192], P('row', ('col', 'layer'))
All inputs are finite; a program needn't handle non-finite values.
Results may differ from a plain program's by a relative error of at most 0.001.
Values may be sent and summed in bfloat16 or wider, within the bound.
A program may use at most 128 MiB of HBM per device.

v0:
```python
import jax
import jax.numpy as jnp
from jax import lax
from jax.sharding import PartitionSpec as P


def partner(x, axis, stride):
    return lax.ppermute(x, axis, [(i, i ^ 1 << stride) for i in range(lax.axis_size(axis))])


def shards(attn_values, out_weight):
    own_half = lax.all_gather(attn_values, "col", axis=1, tiled=True)
    other_part = partner(own_half, "layer", 0)
    first_layer = lax.axis_index("layer") == 0
    lower_half = jnp.where(first_layer, own_half, other_part)
    upper_half = jnp.where(first_layer, other_part, own_half)
    column_pair = lax.all_to_all(out_weight, "layer", split_axis=1, concat_axis=0, tiled=True)
    gathered = lax.all_gather(column_pair, "row", axis=0, tiled=True)
    row_count = lax.axis_size("row")
    depth_rows = out_weight.shape[0]
    stacked = gathered.reshape(row_count, 2, depth_rows, gathered.shape[1])
    weight_lower = stacked[:, 0].reshape(row_count * depth_rows, gathered.shape[1])
    weight_upper = stacked[:, 1].reshape(row_count * depth_rows, gathered.shape[1])
    summed = jnp.dot(lower_half, weight_lower, preferred_element_type=jnp.float32)
    summed = summed + jnp.dot(upper_half, weight_upper, preferred_element_type=jnp.float32)
    projected = summed.astype(jnp.bfloat16)
    return projected


def solution(mesh):
    in_specs = (P("row", ("layer", "col")), P(("layer", "row"), "col"))
    out_specs = P("row", ("col", "layer"))
    return jax.shard_map(shards, mesh=mesh, in_specs=in_specs, out_specs=out_specs, check_vma=False)
```

profile of v0, /device:TPU:0, one launch (start us, length us, event | category | flops | bytes accessed | tf_op | source)
XLA Modules:
  0.0 224.6 jit_solution(15008742448602999398)
XLA Ops:
  6.5 0.0 all-gather.3.cloned.1.call-start
  6.5 0.7 all-gather.3.cloned.1.call-update
  7.3 0.0 all-gather.5.cloned.1.call-start
  7.3 6.5 %copy.3 = bf16[1024,2048]{0,1:T(8,128)(2,1)} copy(bf16[1024,2048]{1,0:T(8,128)(2,1)} %param.3) | data formatting | bytes 8388608 | tf_op args[1]
  13.8 56.3 %all_to_all.19 = bf16[1024,2,1024]{0,2,1:T(8,128)(2,1)} all-to-all(bf16[1024,2,1024]{0,2,1:T(8,128)(2,1)} %bitcast.11), channel_id=1, replica_groups=mesh['row'=4,'col'=4,'layer'=2] {'layer'}, dimensions={1} | all-to-all | bytes 8388608 | tf_op jit(solution)/shard_map/all_to_all | solution.py:17
  70.1 6.3 %copy.4 = bf16[2,1024,1024]{2,1,0:T(8,128)(2,1)} copy(bf16[2,1024,1024]{1,2,0:T(8,128)(2,1)} %bitcast.10) | data formatting | bytes 8388608 | tf_op jit(solution)/shard_map/all_to_all | solution.py:17
  76.3 0.0 all-gather.5.cloned.1.call-update
  76.4 16.0 %all-gather.3.cloned.1.call-done = bf16[512,4096]{1,0:T(8,128)(2,1)} async-done(((bf16[512,1024]{1,0:T(8,128)(2,1)}), bf16[512,4096]{1,0:T(8,128)(2,1)}) %all-gather.3.cloned.1.call-update) | async-done | bytes 4194320 | tf_op jit(solution)/shard_map/all_gather | solution.py:12
  92.4 1.5 collective-permute-start
  93.9 104.5 %all-gather.5.cloned.1.call-done = bf16[8192,1024]{1,0:T(8,128)(2,1)} async-done(((bf16[2048,1024]{1,0:T(8,128)(2,1)}), bf16[8192,1024]{1,0:T(8,128)(2,1)}) %all-gather.5.cloned.1.call-update) | async-done | bytes 16777232 | tf_op jit(solution)/shard_map/all_gather | solution.py:18
  198.4 0.0 copy-start
  198.4 7.0 %fusion.8 = (bf16[4,1,1024,1024]{3,2,1,0:T(8,128)(2,1)S(1)}, bf16[4,1,1024,1024]{3,2,1,0:T(8,128)(2,1)S(1)}) fusion(bf16[4,2,1024,1024]{3,2,1,0:T(8,128)(2,1)} %bitcast.8), kind=kLoop, calls=%fused_computation.7 | loop fusion | bytes 33554432 | tf_op jit(solution)/shard_map/slice | solution.py:22
  205.4 0.0 collective-permute-done
  205.4 0.0 copy-done
  205.4 6.8 %fusion = f32[512,1024]{1,0:T(8,128)S(1)} fusion(bf16[4096,1024]{1,0:T(8,128)(2,1)S(1)} %bitcast.13, bf16[512,4096]{1,0:T(8,128)(2,1)} %collective-permute-done, bf16[512,4096]{1,0:T(8,128)(2,1)S(1)} %copy-done, pred[]{:T(512)S(6)} %eq.3), kind=kOutput, calls=%fused_computation | convolution fusion | flops 4297064448 | bytes 18874368 | tf_op jit(solution)/shard_map/dot_general | solution.py:25
  212.2 5.6 %add_convert_fusion = bf16[512,1024]{1,0:T(8,128)(2,1)} fusion(f32[512,1024]{1,0:T(8,128)S(1)} %fusion, bf16[4096,1024]{1,0:T(8,128)(2,1)S(1)} %bitcast.12, bf16[512,4096]{1,0:T(8,128)(2,1)S(1)} %copy-done, bf16[512,4096]{1,0:T(8,128)(2,1)} %collective-permute-done, pred[]{:T(512)S(6)} %eq.3), kind=kOutput, calls=%fused_computation.6 | convolution fusion | flops 4298113024 | bytes 19922944 | tf_op jit(solution)/shard_map/dot_general | solution.py:24
Async XLA Ops:
  6.5 85.9 %all-gather.3.cloned.1.call-start = ((), (), s32[]{:S(2)}) async-start(), calls=%async_computation.1 | async-start | bytes 5242880 | tf_op jit(solution)/shard_map/all_gather | solution.py:12
  7.3 191.1 %all-gather.5.cloned.1.call-start = ((), (), s32[]{:S(2)}) async-start(), calls=%async_computation.2 | async-start | bytes 20971520 | tf_op jit(solution)/shard_map/all_gather | solution.py:18
  92.4 113.0 %collective-permute-start = (bf16[512,4096]{1,0:T(8,128)(2,1)}, bf16[512,4096]{1,0:T(8,128)(2,1)}, u32[]{:S(2)}, u32[]{:S(2)}) collective-permute-start(bf16[512,4096]{1,0:T(8,128)(2,1)} %all-gather.3.cloned.1.call-done), channel_id=1, source_target_pairs={{0,1},{1,0},{2,3},{3,2},{4,5},{5,4},{6,7},{7,6},{8,9},{9,8},{10,11... | collective-permute-start | bytes 12582920 | tf_op jit(solution)/shard_map/ppermute | solution.py:8
  198.4 7.1 %copy-start = (bf16[512,4096]{1,0:T(8,128)(2,1)S(1)}, bf16[512,4096]{1,0:T(8,128)(2,1)}, u32[]{:S(2)}) copy-start(bf16[512,4096]{1,0:T(8,128)(2,1)} %all-gather.3.cloned.1.call-done) | copy-start | bytes 12582916
Sparse Core Ops, SparseCore 0:
  8.9 83.4 all-gather.2
  93.9 104.3 all-gather.4
where the time goes:
time: 225 us
  waiting for transfers between devices  121 us (54%)
  blocking collectives  56.3 us (25%)
  local copies, waits for them, and re-layouts  19.8 us (9%)
  between operations  13.4 us (6%)
  matrix products  12.4 us (6%)
    all_gather x1, waiting for transfers between devices, shards(): gathered = lax.all_gather(column_pair, 'row', axis=0, tiled=True)  104 us
    all_to_all x1, blocking collectives, shards(): lax.all_to_all(out_weight, 'layer', split_axis=1, concat_axis=0, tiled=True)  56.3 us
    all_gather x1, waiting for transfers between devices, shards(): own_half = lax.all_gather(attn_values, 'col', axis=1, tiled=True)  16 us
    slice x1, local copies, waits for them, and re-layouts, shards(): stacked[:, 0].reshape(row_count * depth_rows, gathered.shape[1])  6.99 us
    dot_general x1, matrix products, shards(): jnp.dot(upper_half, weight_upper, preferred_element_type=jnp.float32)  6.79 us
    unnamed x3, local copies, waits for them, and re-layouts  6.5 us
    all_to_all x1, local copies, waits for them, and re-layouts, shards(): lax.all_to_all(out_weight, 'layer', split_axis=1, concat_axis=0, tiled=True)  6.26 us
    dot_general x1, matrix products, shards(): jnp.dot(lower_half, weight_lower, preferred_element_type=jnp.float32)  5.57 us
  transfers between devices with their start and end apart: 3, of which 2 were waited for; matrix products, arithmetic and copies ran while one was open for 9% of the time, Pallas kernels for 0%

commit v1 on v0

v1 whole, which is shorter than its diff:
```python
import functools

import jax
import jax.numpy as jnp
from jax import lax
from jax.experimental import pallas as pl
from jax.experimental.pallas import tpu as pltpu
from jax.sharding import PartitionSpec as P

TOKEN_CHUNKS = 4
COLUMN_CHUNKS = 8


def schedule(token_chunks, column_chunks, col_count):
    events = []
    for t in range(token_chunks):
        for d in range(1, col_count):
            at = (col_count - 1) * t + (1 if d == 1 else d + 1)
            events.append((at, 0, t, d))
    span = (col_count - 1) * token_chunks * 4 / 3
    for j in range(column_chunks):
        events.append((span * (j + 1) / column_chunks, 1, j, 0))
    ordered, clock = [], 0
    for at, kind, first, second in sorted(events, key=lambda e: (e[1], e[2], e[3])):
        if kind == 0:
            clock = max(clock, at)
            at = clock
        ordered.append((at, kind, first, second))
    return sorted(ordered)


def kernel(rows, cols, a_ref, w_ref, o_ref, abuf, wbuf, ysend, yrecv, loc_a, loc_w, a_recv, a_right, a_left, w_recv, w_send, p_send, y_recv, y_send):
    r, c, l = lax.axis_index("row"), lax.axis_index("col"), lax.axis_index("layer")
    groups = rows // 2
    core, group = lax.rem(r, 2), r // 2
    partner = 2 * group + 1 - core
    tokens, depth_a = a_ref.shape
    depth_w, width = w_ref.shape
    tt, half = tokens // TOKEN_CHUNKS, width // 2
    nc, jh = width // COLUMN_CHUNKS, COLUMN_CHUNKS // 2

    def peer(g):
        return 2 * lax.rem(group + g + groups, groups) + core

    def a_at(block, t):
        return abuf.at[block, pl.ds(t * tt, tt), :]

    def w_at(row, j):
        return wbuf.at[j, pl.ds(pl.multiple_of(row * depth_w, depth_w), depth_w), :]

    def own_a(t):
        return pltpu.make_async_copy(a_ref.at[pl.ds(t * tt, tt), :], a_at(c, t), loc_a.at[t])

    def own_w(j):
        side = 1 - l if j < jh else l
        at = pl.multiple_of(side * half + (j % jh) * nc, nc)
        return pltpu.make_async_copy(w_ref.at[:, pl.ds(at, nc)], w_at(r, j), loc_w.at[j])

    def a_copy(block, t, to, sems):
        return pltpu.make_async_remote_copy(a_at(block, t), a_at(block, t), sems.at[t, block], a_recv.at[t, block], device_id={"col": to})

    def w_copy(row, j, to, sem):
        return pltpu.make_async_remote_copy(w_at(row, j), w_at(row, j), sem, w_recv.at[j, row], device_id={"row": to})

    def y_copy(t, j):
        rows_t = pl.ds(t * tt, tt)
        return pltpu.make_async_remote_copy(ysend.at[j, rows_t, :], yrecv.at[j, rows_t, :], y_send.at[t, j], y_recv.at[t, j], device_id={"layer": 1 - l})

    def right(block, t):
        return a_copy(block, t, c + 1, a_right)

    def left(block, t):
        return a_copy(block, t, c - 1, a_left)

    for n in range(max(TOKEN_CHUNKS, COLUMN_CHUNKS)):
        if n < TOKEN_CHUNKS:
            own_a(n).start()
        if n < COLUMN_CHUNKS:
            own_w(n).start()

    has_right, has_left = c < cols - 1, c > 0
    barrier = pltpu.get_barrier_semaphore()

    def greet(device_id):
        pl.semaphore_signal(barrier, inc=1, device_id=device_id)

    greet({"row": partner})
    greet({"layer": 1 - l})
    for g in range(1, groups):
        greet({"row": peer(g)})
    pl.when(has_right)(lambda: greet({"col": c + 1}))
    pl.when(has_left)(lambda: greet({"col": c - 1}))
    pl.semaphore_wait(barrier, 1 + groups + has_right.astype(jnp.int32) + has_left.astype(jnp.int32))

    def send_a(t):
        own_a(t).wait()
        pl.when(has_right)(lambda: right(c, t).start())
        pl.when(has_left)(lambda: left(c, t).start())

    def send_w(j):
        own_w(j).wait()
        for g in range(1, groups):
            w_copy(r, j, peer(g), w_send.at[j, g]).start()
        w_copy(r, j, partner, p_send.at[j, 0]).start()

    send_a(0)
    send_w(0)
    send_a(1)
    for j in range(1, COLUMN_CHUNKS):
        send_w(j)

    def take_a(t, d):
        @pl.when(c >= d)
        def _():
            right(c - d, t).wait_recv()
            pl.when(has_right)(lambda: right(c - d, t).start())

        @pl.when(c + d < cols)
        def _():
            left(c + d, t).wait_recv()
            pl.when(has_left)(lambda: left(c + d, t).start())

        if d == cols - 1 and t + 2 < TOKEN_CHUNKS:
            send_a(t + 2)

    def take_w(j):
        for g in range(1, groups):
            source = peer(-g)
            w_copy(source, j, partner, p_send.at[j, g]).wait_recv()
            w_copy(source, j, partner, p_send.at[j, g]).start()

    def take_partner(j):
        for g in range(groups):
            source = 2 * g + 1 - core
            w_copy(source, j, partner, p_send.at[j, 0]).wait_recv()

    def product(rows_t, j):
        total = jnp.dot(abuf[0, rows_t, :], wbuf[j, pl.ds(0, depth_a), :], preferred_element_type=jnp.float32)
        for block in range(1, cols):
            total += jnp.dot(abuf[block, rows_t, :], wbuf[j, pl.ds(block * depth_a, depth_a), :], preferred_element_type=jnp.float32)
        return total

    def partials(tiles):
        t0, j0 = tiles[0]
        wide = 1 + tiles[-1][1] - j0

        def one(n, carry):
            t, j = t0 + n // wide, j0 + lax.rem(n, wide)
            rows_t = pl.ds(pl.multiple_of(t * tt, tt), tt)
            ysend[j, rows_t, :] = product(rows_t, j)
            return carry

        def send(n, carry):
            y_copy(t0 + n // wide, j0 + lax.rem(n, wide)).start()
            return carry

        lax.fori_loop(0, len(tiles), one, 0)
        lax.fori_loop(0, len(tiles), send, 0)

    def finish(j):
        def one(t, carry):
            rows_t = pl.ds(pl.multiple_of(t * tt * 2, tt * 2), tt * 2)
            y_copy(2 * t, j - jh).wait_recv()
            y_copy(2 * t + 1, j - jh).wait_recv()
            o_ref[rows_t, (j - jh) * nc:(j - jh + 1) * nc] = (product(rows_t, j) + yrecv[j - jh, rows_t, :]).astype(o_ref.dtype)
            return carry

        lax.fori_loop(0, TOKEN_CHUNKS // 2, one, 0)

    got_t, got_j, done_own = 0, 0, jh
    for _, kind, first, second in schedule(TOKEN_CHUNKS, COLUMN_CHUNKS, cols):
        if kind == 0:
            take_a(first, second)
            if second == cols - 1:
                got_t = first + 1
                if got_j:
                    partials([(first, j) for j in range(min(got_j, jh))])
        else:
            take_w(first)
            take_partner(first)
            got_j = first + 1
            if first < jh and got_t:
                partials([(t, first) for t in range(got_t)])
        while got_t == TOKEN_CHUNKS and done_own < got_j:
            finish(done_own)
            done_own += 1

    for t in range(TOKEN_CHUNKS):
        for block in range(cols):
            @pl.when(has_right & (block <= c))
            def _():
                right(block, t).wait_send()

            @pl.when(has_left & (block >= c))
            def _():
                left(block, t).wait_send()

        for j in range(jh):
            y_copy(t, j).wait_send()
    for j in range(COLUMN_CHUNKS):
        for g in range(groups):
            w_copy(r, j, partner, p_send.at[j, g]).wait_send()
            if g:
                w_copy(r, j, partner, w_send.at[j, g]).wait_send()


def solution(mesh):
    rows, cols = mesh.shape["row"], mesh.shape["col"]

    def shards(attn_values, out_weight):
        tokens, depth_a = attn_values.shape
        depth_w, width = out_weight.shape
        nc, jh = width // COLUMN_CHUNKS, COLUMN_CHUNKS // 2
        dma = pltpu.SemaphoreType.DMA
        return pl.pallas_call(
            functools.partial(kernel, rows, cols),
            out_shape=jax.ShapeDtypeStruct((tokens, width // 2), jnp.bfloat16),
            in_specs=[pl.BlockSpec(memory_space=pl.ANY)] * 2,
            out_specs=pl.BlockSpec(memory_space=pltpu.VMEM),
            scratch_shapes=[
                pltpu.VMEM((cols, tokens, depth_a), jnp.bfloat16),
                pltpu.VMEM((COLUMN_CHUNKS, rows * depth_w, nc), jnp.bfloat16),
                pltpu.VMEM((jh, tokens, nc), jnp.float32),
                pltpu.VMEM((jh, tokens, nc), jnp.float32),
                dma((TOKEN_CHUNKS,)),
                dma((COLUMN_CHUNKS,)),
                dma((TOKEN_CHUNKS, cols)),
                dma((TOKEN_CHUNKS, cols)),
                dma((TOKEN_CHUNKS, cols)),
                dma((COLUMN_CHUNKS, rows)),
                dma((COLUMN_CHUNKS, rows // 2)),
                dma((COLUMN_CHUNKS, rows // 2)),
                dma((TOKEN_CHUNKS, jh)),
                dma((TOKEN_CHUNKS, jh)),
            ],
            compiler_params=pltpu.CompilerParams(collective_id=0, has_side_effects=True, vmem_limit_bytes=48 * 2**20),
        )(attn_values, out_weight)

    in_specs = (P("row", ("layer", "col")), P(("layer", "row"), "col"))
    out_specs = P("row", ("col", "layer"))
    return jax.shard_map(shards, mesh=mesh, in_specs=in_specs, out_specs=out_specs, check_vma=False)
```

time: 225 us -> 102 us (0.45)
  waiting for transfers between devices: 121 us -> 0 us
  Pallas kernels: 0 us -> 98.3 us
  blocking collectives: 56.3 us -> 0 us
  local copies, waits for them, and re-layouts: 19.8 us -> 2.2 us
  between operations: 13.4 us -> 0.01 us
  matrix products: 12.4 us -> 0 us
    all_gather x2 -> x0, waiting for transfers between devices: 121 us -> none  [the longest x1 104 us: shards(): gathered = lax.all_gather(column_pair, 'row', axis=0, tiled=True)]
    pallas_call x0 -> x1, Pallas kernels: none -> 98.3 us  [shards(): pl.pallas_call(functools.partial(kernel, rows, cols), out_shape=jax.Shape...]
    all_to_all x1 -> x0, blocking collectives: 56.3 us -> none  [shards(): lax.all_to_all(out_weight, 'layer', split_axis=1, concat_axis=0, tiled=True)]
    dot_general x2 -> x0, matrix products: 12.4 us -> none  [the longest x1 6.79 us: shards(): jnp.dot(upper_half, weight_upper, preferred_element_type=jnp.float32)]
    slice x1 -> x0, local copies, waits for them, and re-layouts: 6.99 us -> none  [shards(): stacked[:, 0].reshape(row_count * depth_rows, gathered.shape[1])]
    all_to_all x1 -> x0, local copies, waits for them, and re-layouts: 6.26 us -> none  [shards(): lax.all_to_all(out_weight, 'layer', split_axis=1, concat_axis=0, tiled=True)]
    unnamed x3, local copies, waits for them, and re-layouts: 6.5 us -> 2.2 us
  transfers between devices with their start and end apart: 3 -> 0, of which waited for: 2 -> 0; matrix products, arithmetic and copies ran while one was open for 9% -> 0% of each run, Pallas kernels for 0% -> 0%
where the time goes in v1:
time: 102 us; the launch traced here: 100 us
  Pallas kernels  98.3 us (96%)
  local copies, waits for them, and re-layouts  2.2 us (2%)
    pallas_call x1, Pallas kernels, shards(): pl.pallas_call(functools.partial(kernel, rows, cols), out_shape=jax.Shape...  98.3 us
    unnamed x3, local copies, waits for them, and re-layouts  2.2 us

profile of v1, /device:TPU:0, one launch (start us, length us, event | category | flops | bytes accessed | tf_op | source)
XLA Modules:
  0.0 100.5 jit_solution(16989575070839779688)
XLA Ops:
  0.0 0.0 copy-start
  0.0 1.2 %copy-done = bf16[512,1024]{1,0:T(8,128)(2,1)S(1)} copy-done((bf16[512,1024]{1,0:T(8,128)(2,1)S(1)}, bf16[512,1024]{1,0:T(8,128)(2,1)}, u32[]{:S(2)}) %copy-start) | copy-done | bytes 1048600
  1.2 98.3 %shard_map.28 = bf16[512,1024]{1,0:T(8,128)(2,1)S(1)} custom-call(bf16[512,1024]{1,0:T(8,128)(2,1)S(1)} %copy-done, bf16[1024,2048]{1,0:T(8,128)(2,1)} %w_ref.1), custom_call_target="tpu_custom_call" | custom-call | tf_op jit(solution)/shard_map/pallas_call | solution.py:215
  99.5 1.0 copy.4
Async XLA Ops:
  0.0 1.2 %copy-start = (bf16[512,1024]{1,0:T(8,128)(2,1)S(1)}, bf16[512,1024]{1,0:T(8,128)(2,1)}, u32[]{:S(2)}) copy-start(bf16[512,1024]{1,0:T(8,128)(2,1)} %a_ref.1) | copy-start | bytes 3145732

commit v2 on v1

--- a/solution.py
+++ b/solution.py
@@ -9,6 +9,10 @@
 
 TOKEN_CHUNKS = 4
 COLUMN_CHUNKS = 8
+
+
+def last_pieces(depth_w):
+    return max(1, min(4, depth_w // 256))
 
 
 def schedule(token_chunks, column_chunks, col_count):
@@ -18,7 +22,7 @@
             at = (col_count - 1) * t + (1 if d == 1 else d + 1)
             events.append((at, 0, t, d))
     span = (col_count - 1) * token_chunks * 4 / 3
-    for j in range(column_chunks):
+    for j in range(column_chunks - 1):
         events.append((span * (j + 1) / column_chunks, 1, j, 0))
     ordered, clock = [], 0
     for at, kind, first, second in sorted(events, key=lambda e: (e[1], e[2], e[3])):
@@ -29,7 +33,7 @@
     return sorted(ordered)
 
 
-def kernel(rows, cols, a_ref, w_ref, o_ref, abuf, wbuf, ysend, yrecv, loc_a, loc_w, a_recv, a_right, a_left, w_recv, w_send, p_send, y_recv, y_send):
+def kernel(rows, cols, a_ref, w_ref, o_ref, abuf, wbuf, ysend, yrecv, early, loc_a, loc_w, a_recv, a_right, a_left, w_recv, w_send, p_send, y_recv, y_send):
     r, c, l = lax.axis_index("row"), lax.axis_index("col"), lax.axis_index("layer")
     groups = rows // 2
     core, group = lax.rem(r, 2), r // 2
@@ -38,6 +42,11 @@
     depth_w, width = w_ref.shape
     tt, half = tokens // TOKEN_CHUNKS, width // 2
     nc, jh = width // COLUMN_CHUNKS, COLUMN_CHUNKS // 2
+    last, cuts = COLUMN_CHUNKS - 1, last_pieces(depth_w)
+    pieces = last + cuts
+
+    def piece(p):
+        return (p, 0, depth_w) if p < last else (last, (p - last) * depth_w // cuts, depth_w // cuts)
 
     def peer(g):
         return 2 * lax.rem(group + g + groups, groups) + core
@@ -45,16 +54,18 @@
     def a_at(block, t):
         return abuf.at[block, pl.ds(t * tt, tt), :]
 
-    def w_at(row, j):
-        return wbuf.at[j, pl.ds(pl.multiple_of(row * depth_w, depth_w), depth_w), :]
+    def w_at(row, p):
+        j, start, count = piece(p)
+        return wbuf.at[j, pl.ds(pl.multiple_of(row * depth_w + start, count), count), :]
 
     def own_a(t):
         return pltpu.make_async_copy(a_ref.at[pl.ds(t * tt, tt), :], a_at(c, t), loc_a.at[t])
 
-    def own_w(j):
+    def own_w(p):
+        j, start, count = piece(p)
         side = 1 - l if j < jh else l
         at = pl.multiple_of(side * half + (j % jh) * nc, nc)
-        return pltpu.make_async_copy(w_ref.at[:, pl.ds(at, nc)], w_at(r, j), loc_w.at[j])
+        return pltpu.make_async_copy(w_ref.at[pl.ds(start, count), pl.ds(at, nc)], w_at(r, p), loc_w.at[p])
 
     def a_copy(block, t, to, sems):
         return pltpu.make_async_remote_copy(a_at(block, t), a_at(block, t), sems.at[t, block], a_recv.at[t, block], device_id={"col": to})
@@ -72,11 +83,11 @@
     def left(block, t):
         return a_copy(block, t, c - 1, a_left)
 
-    for n in range(max(TOKEN_CHUNKS, COLUMN_CHUNKS)):
+    for n in range(max(TOKEN_CHUNKS, pieces)):
+        if n < pieces:
+            own_w(n).start()
         if n < TOKEN_CHUNKS:
             own_a(n).start()
-        if n < COLUMN_CHUNKS:
-            own_w(n).start()
 
     has_right, has_left = c < cols - 1, c > 0
     barrier = pltpu.get_barrier_semaphore()
@@ -103,11 +114,11 @@
             w_copy(r, j, peer(g), w_send.at[j, g]).start()
         w_copy(r, j, partner, p_send.at[j, 0]).start()
 
+    send_w(0)
     send_a(0)
-    send_w(0)
     send_a(1)
-    for j in range(1, COLUMN_CHUNKS):
-        send_w(j)
+    for p in range(1, pieces):
+        send_w(p)
 
     def take_a(t, d):
         @pl.when(c >= d)
@@ -167,7 +178,52 @@
 
         lax.fori_loop(0, TOKEN_CHUNKS // 2, one, 0)
 
-    got_t, got_j, done_own = 0, 0, jh
+    def part(j, rows_t, start, count):
+        columns = pl.ds(pl.multiple_of(lax.rem(start, depth_a), min(count, depth_a)), count)
+        weights = wbuf[j, pl.ds(pl.multiple_of(start, count), count), :]
+        return jnp.dot(abuf[start // depth_a, rows_t, columns], weights, preferred_element_type=jnp.float32)
+
+    def each_rows(body):
+        def one(t, carry):
+            body(pl.ds(pl.multiple_of(t * tt * 2, tt * 2), tt * 2))
+            return carry
+
+        lax.fori_loop(0, TOKEN_CHUNKS // 2, one, 0)
+
+    def take_own_rows():
+        for h in range(cuts):
+            w_copy(partner, last + h, partner, p_send.at[last + h, 0]).wait_recv()
+        count = min(depth_w, depth_a)
+        for n in range(depth_w // count):
+            @each_rows
+            def _(rows_t):
+                total = part(last, rows_t, r * depth_w + n * count, count) + part(last, rows_t, partner * depth_w + n * count, count)
+                early[rows_t, :] = total if n == 0 else early[rows_t, :] + total
+
+    def finish_last():
+        count = depth_w // cuts
+        for t in range(TOKEN_CHUNKS):
+            y_copy(t, jh - 1).wait_recv()
+        for h in range(cuts):
+            take_w(last + h)
+            for g in range(1, groups):
+                own, other = peer(-g), peer(-g) + 1 - 2 * core
+
+                @each_rows
+                def _(rows_t):
+                    early[rows_t, :] += part(last, rows_t, own * depth_w + h * count, count)
+
+                w_copy(other, last + h, partner, p_send.at[last + h, 0]).wait_recv()
+
+                @each_rows
+                def _(rows_t):
+                    total = early[rows_t, :] + part(last, rows_t, other * depth_w + h * count, count)
+                    if h < cuts - 1 or g < groups - 1:
+                        early[rows_t, :] = total
+                    else:
+                        o_ref[rows_t, (jh - 1) * nc:jh * nc] = (total + yrecv[jh - 1, rows_t, :]).astype(o_ref.dtype)
+
+    got_t, got_j, done_own, own_rows = 0, 0, jh, False
     for _, kind, first, second in schedule(TOKEN_CHUNKS, COLUMN_CHUNKS, cols):
         if kind == 0:
             take_a(first, second)
@@ -176,6 +232,9 @@
                 if got_j:
                     partials([(first, j) for j in range(min(got_j, jh))])
         else:
+            if first == last - 1 and got_t == TOKEN_CHUNKS:
+                take_own_rows()
+                own_rows = True
             take_w(first)
             take_partner(first)
             got_j = first + 1
@@ -184,6 +243,9 @@
         while got_t == TOKEN_CHUNKS and done_own < got_j:
             finish(done_own)
             done_own += 1
+    if not own_rows:
+        take_own_rows()
+    finish_last()
 
     for t in range(TOKEN_CHUNKS):
         for block in range(cols):
@@ -197,11 +259,11 @@
 
         for j in range(jh):
             y_copy(t, j).wait_send()
-    for j in range(COLUMN_CHUNKS):
+    for p in range(pieces):
         for g in range(groups):
-            w_copy(r, j, partner, p_send.at[j, g]).wait_send()
+            w_copy(r, p, partner, p_send.at[p, g]).wait_send()
             if g:
-                w_copy(r, j, partner, w_send.at[j, g]).wait_send()
+                w_copy(r, p, partner, w_send.at[p, g]).wait_send()
 
 
 def solution(mesh):
@@ -211,30 +273,32 @@
         tokens, depth_a = attn_values.shape
         depth_w, width = out_weight.shape
         nc, jh = width // COLUMN_CHUNKS, COLUMN_CHUNKS // 2
+        pieces = COLUMN_CHUNKS - 1 + last_pieces(depth_w)
         dma = pltpu.SemaphoreType.DMA
         return pl.pallas_call(
             functools.partial(kernel, rows, cols),
             out_shape=jax.ShapeDtypeStruct((tokens, width // 2), jnp.bfloat16),
-            in_specs=[pl.BlockSpec(memory_space=pl.ANY)] * 2,
+            in_specs=[pl.BlockSpec(memory_space=pltpu.HBM)] * 2,
             out_specs=pl.BlockSpec(memory_space=pltpu.VMEM),
             scratch_shapes=[
                 pltpu.VMEM((cols, tokens, depth_a), jnp.bfloat16),
                 pltpu.VMEM((COLUMN_CHUNKS, rows * depth_w, nc), jnp.bfloat16),
                 pltpu.VMEM((jh, tokens, nc), jnp.float32),
                 pltpu.VMEM((jh, tokens, nc), jnp.float32),
+                pltpu.VMEM((tokens, nc), jnp.float32),
                 dma((TOKEN_CHUNKS,)),
-                dma((COLUMN_CHUNKS,)),
+                dma((pieces,)),
                 dma((TOKEN_CHUNKS, cols)),
                 dma((TOKEN_CHUNKS, cols)),
                 dma((TOKEN_CHUNKS, cols)),
-                dma((COLUMN_CHUNKS, rows)),
-                dma((COLUMN_CHUNKS, rows // 2)),
-                dma((COLUMN_CHUNKS, rows // 2)),
+                dma((pieces, rows)),
+                dma((pieces, rows // 2)),
+                dma((pieces, rows // 2)),
                 dma((TOKEN_CHUNKS, jh)),
                 dma((TOKEN_CHUNKS, jh)),
             ],
             compiler_params=pltpu.CompilerParams(collective_id=0, has_side_effects=True, vmem_limit_bytes=48 * 2**20),
-        )(attn_values, out_weight)
+        )(*(pltpu.with_memory_space_constraint(x, pltpu.HBM) for x in (attn_values, out_weight)))
 
     in_specs = (P("row", ("layer", "col")), P(("layer", "row"), "col"))
     out_specs = P("row", ("col", "layer"))

time: 102 us -> 99.6 us (0.976); the launches traced: 100 us -> 99.5 us
  local copies, waits for them, and re-layouts: 2.2 us -> 0.97 us
    unnamed x3 -> x1, local copies, waits for them, and re-layouts: 2.2 us -> 0.97 us
where the time goes in v2:
time: 99.6 us; the launch traced here: 99.5 us
  Pallas kernels  98.5 us (99%)
    pallas_call x1, Pallas kernels, shards(): pl.pallas_call(functools.partial(kernel, rows, cols), out_shape=jax.Shape...  98.5 us

profile of v2, /device:TPU:0, one launch (start us, length us, event | category | flops | bytes accessed | tf_op | source)
XLA Modules:
  0.0 99.5 jit_solution(3855061594775070620)
XLA Ops:
  0.0 98.5 %shard_map.28 = bf16[512,1024]{1,0:T(8,128)(2,1)S(1)} custom-call(bf16[512,1024]{1,0:T(8,128)(2,1)} %a_ref.1, bf16[1024,2048]{1,0:T(8,128)(2,1)} %w_ref.1), custom_call_target="tpu_custom_call" | custom-call | tf_op jit(solution)/shard_map/pallas_call | solution.py:278
  98.5 1.0 copy.4

commit v3 on v2

--- a/solution.py
+++ b/solution.py
@@ -12,7 +12,7 @@
 
 
 def last_pieces(depth_w):
-    return max(1, min(4, depth_w // 256))
+    return max(1, min(8, depth_w // 128))
 
 
 def schedule(token_chunks, column_chunks, col_count):

time: 99.6 us -> 105 us (1.054)
  Pallas kernels: 98.5 us -> 104 us
    pallas_call x1, Pallas kernels: 98.5 us -> 104 us  [shards(): pl.pallas_call(functools.partial(kernel, rows, cols), out_shape=jax.Shape...]
where the time goes in v3:
time: 105 us
  Pallas kernels  104 us (99%)
    pallas_call x1, Pallas kernels, shards(): pl.pallas_call(functools.partial(kernel, rows, cols), out_shape=jax.Shape...  104 us

profile of v3, /device:TPU:0, one launch (start us, length us, event | category | flops | bytes accessed | tf_op | source)
XLA Modules:
  0.0 104.7 jit_solution(14362353716256457971)
XLA Ops:
  0.0 103.8 %shard_map.28 = bf16[512,1024]{1,0:T(8,128)(2,1)S(1)} custom-call(bf16[512,1024]{1,0:T(8,128)(2,1)} %a_ref.1, bf16[1024,2048]{1,0:T(8,128)(2,1)} %w_ref.1), custom_call_target="tpu_custom_call" | custom-call | tf_op jit(solution)/shard_map/pallas_call | solution.py:278
  103.8 1.0 copy.4
